TPU v7x, 32 devices: a whole 2x2x4 slice. The times are simulated.
32 devices in a mesh: img: 2 (over y), sub: 4 (over z), rng: 4 (over x, core).
Axes of the slice: x: 2, y: 2, z: 4, core: 2. Of those that a mesh axis runs over, the one named last changes fastest.
Arguments:
- image: bfloat16 [2, 16, 128, 4096], P(None, ('img', 'sub'), None, 'rng'), parts along dimension 1, may hold values from -6 to 6
- interp_weights: bfloat16 [4, 2, 2, 2, 128, 128], replicated, may hold values from -0.25 to 0.25
- range_taps: float32 [4, 4], replicated, may hold values from -2 to 2
- range_shifts: int32 [4, 2, 128], replicated, may hold values from -8 to 5
Outputs:
- merged_image: bfloat16 [2, 16, 128, 4096], P(None, ('img', 'sub'), None, 'rng'), parts along dimension 1
There are 2 independent parts, one for each index of `img`. A program takes and returns all parts, laid end to end along the dimension named above; an argument that names none is the same for every part. Nothing has to cross between parts.
All inputs are finite; a program needn't handle non-finite values.
Results may differ from a plain program's by a relative error of at most 0.0095.
Values may be sent and summed in bfloat16 or wider, within the bound.
A program may use at most 64 MiB of HBM per device.

v0:
```python
import math

import jax
import jax.numpy as jnp
from jax import lax
from jax.sharding import PartitionSpec as P

ANGLES = 128
RANGE = 4096
RIM = 8
TAPS = 4
LEVELS = 4


phase_step = 2.0 * math.pi / 64.0


def padded_2(cells, sides, width):
    for axis, dim in sides:
        count = lax.axis_size(axis)
        ends = count - 1
        head = lax.slice_in_dim(cells, 0, width, axis=dim)
        tail = lax.slice_in_dim(cells, cells.shape[dim] - width, cells.shape[dim], axis=dim)
        cells = jnp.concatenate(
            [
                lax.ppermute(tail, axis, [(i, (i + 1) % count) for i in range(ends)]),
                cells,
                lax.ppermute(head, axis, [((i + 1) % count, i) for i in range(ends)]),
            ],
            axis=dim,
        )
    return cells


def from_partner(value, axis, stride):
    mask = 2**stride
    pairs = [(source, source ^ mask) for source in range(lax.axis_size(axis))]
    return lax.ppermute(value, axis, pairs)


def rotate(merged_sum, level_index, half_index, range_start, range_width):
    angle_rows = half_index * ANGLES + jnp.arange(ANGLES, dtype=jnp.int32)
    range_cols = range_start + jnp.arange(range_width, dtype=jnp.int32)
    wrapped = range_cols[None, :] * (angle_rows[:, None] + 1) * (7 + level_index) % 64
    phase = wrapped.astype(jnp.float32) * phase_step
    cosine = jnp.cos(phase)
    sinus = jnp.sin(phase)
    return jnp.stack(
        [
            merged_sum[0] * cosine - merged_sum[1] * sinus,
            merged_sum[0] * sinus + merged_sum[1] * cosine,
        ]
    )


def level_coef(range_taps, range_shifts, level_index, side_index):
    offsets = jnp.arange(2 * RIM + 1, dtype=jnp.int32) - RIM
    tap_ids = jnp.arange(TAPS, dtype=jnp.int32)
    hits = (
        range_shifts[level_index, side_index][:, None, None] + tap_ids[None, :, None]
        == offsets[None, None, :]
    )
    return jnp.einsum(
        "t,ato->ao",
        range_taps[level_index],
        hits.astype(jnp.float32),
        precision=lax.Precision.HIGHEST,
    )


def interpolate(padded, coef, range_width):
    total = None
    for offset_index in range(2 * RIM + 1):
        term = coef[:, offset_index, None] * padded[
            ..., offset_index : offset_index + range_width
        ].astype(jnp.float32)
        total = term if total is None else total + term
    return total.astype(jnp.bfloat16)


def block_of(weight_pair):
    return jnp.stack(
        [jnp.stack([weight_pair[0], -weight_pair[1]]), jnp.stack([weight_pair[1], weight_pair[0]])]
    )


def combine_sides(lower_rows, upper_rows, weights_level, half_index):
    chosen = lax.dynamic_index_in_dim(weights_level, half_index, 1, keepdims=False)
    merged_sum = None
    for side_index, source in ((0, lower_rows), (1, upper_rows)):
        product = jnp.einsum(
            "xcij,cgjr->xgir",
            block_of(chosen[side_index]),
            source,
            preferred_element_type=jnp.float32,
        )
        merged_sum = product if merged_sum is None else merged_sum + product
    return merged_sum


def on_device(image, interp_weights, range_taps, range_shifts):
    range_width = image.shape[3]
    sub_count = lax.axis_size("sub")
    bit_count = sub_count.bit_length() - 1
    sub_index = lax.axis_index("sub")
    range_start = lax.axis_index("rng") * range_width
    current = padded_2(image, (("rng", 3),), LEVELS * RIM)
    margin = LEVELS * RIM
    for level_index in range(LEVELS):
        bit = level_index % bit_count
        own_half = sub_index // 2**bit % 2
        padded = current
        margin = margin - RIM
        out_width = range_width + 2 * margin
        coef = jnp.where(
            own_half == 0,
            level_coef(range_taps, range_shifts, level_index, 0),
            level_coef(range_taps, range_shifts, level_index, 1),
        )
        own_rows = interpolate(padded, coef, out_width)
        partner = from_partner(own_rows, "sub", bit)
        lower_rows = jnp.where(own_half == 0, own_rows, partner)
        upper_rows = jnp.where(own_half == 0, partner, own_rows)
        merged = combine_sides(lower_rows, upper_rows, interp_weights[level_index], own_half)
        turned = rotate(merged, level_index, own_half, range_start - margin, out_width)
        global_cols = range_start - margin + jnp.arange(out_width, dtype=jnp.int32)
        inside = jnp.logical_and(global_cols >= 0, global_cols < RANGE)
        turned = jnp.where(inside, turned, 0.0)
        current = turned.astype(jnp.bfloat16)
    return current


def solution(mesh):
    return jax.shard_map(
        on_device,
        mesh=mesh,
        in_specs=(P(None, ("img", "sub"), None, "rng"), P(), P(), P()),
        out_specs=P(None, ("img", "sub"), None, "rng"),
        check_vma=False,
    )
```

profile of v0, /device:TPU:0, one launch (start us, length us, event | category | flops | bytes accessed | tf_op | source)
XLA Modules:
  0.0 204.4 jit_solution(337052777099542682)
XLA Ops:
  0.0 1.7 copy.8
  1.7 1.3 collective-permute-start.1
  3.0 3.0 %collective-permute-start = (bf16[2,2,128,32]{2,3,1,0:T(8,128)(2,1)S(1)}, bf16[2,2,128,32]{2,3,1,0:T(8,128)(2,1)S(1)}, u32[]{:S(2)}, u32[]{:S(2)}) collective-permute-start(bf16[2,2,128,32]{2,3,1,0:T(8,128)(2,1)S(1)} %get-tuple-element.49), channel_id=1, source_target_pairs={{0,1},{1,2},{2,3},{4,5},{5,6},{6,7},{8,9},{9,10},{10,11},{12,13},{... | collective-permute-start | bytes 98312 | tf_op jit(solution)/shard_map/ppermute | solution.py:26
  9.3 2.5 %select_reduce_fusion.6 = (f32[128,17]{1,0:T(8,128)}, f32[128,17]{1,0:T(8,128)}, f32[128,17]{1,0:T(8,128)}, f32[128,17]{1,0:T(8,128)}, f32[128,17]{1,0:T(8,128)}...) fusion(f32[4]{0:T(128)S(1)} %get-tuple-element.169, s32[128,4]{1,0:T(8,128)S(1)} %get-tuple-element.177, ...), kind=kLoop, calls=%fused_computation.96 | loop fusion | flops 191488 | bytes 86148
  13.2 0.7 dynamic-slice_bitcast_fusion.1
  17.9 4.7 %add_convert_fusion = bf16[2,2,128,1072]{2,3,1,0:T(8,128)(2,1)S(1)} fusion(bf16[2,2,128,1088]{2,3,1,0:T(8,128)(2,1)S(1)} %pad_maximum_fusion, f32[128]{0:T(128)S(1)} %get-tuple-element.135, f32[128]{0:T(128)S(1)} %get-tuple-element.136, f32[128]{0:T(128)S(1)} %get-tuple-element.137, f32[128]{0:T(128)S(1)} %get-tuple-element.138, ...), kind=kLoop, calls=%fused_computation.14 | loop fusion | flops 27992064 | bytes 19767808 | tf_op jit(solution)/shard_map/convert_element_type | solution.py:78
  22.7 3.1 %collective-permute-start.2 = (bf16[2,2,128,1072]{2,3,1,0:T(8,128)(2,1)S(1)}, bf16[2,2,128,1072]{2,3,1,0:T(8,128)(2,1)S(1)}, u32[]{:S(2)}, u32[]{:S(2)}) collective-permute-start(bf16[2,2,128,1072]{2,3,1,0:T(8,128)(2,1)S(1)} %add_convert_fusion), channel_id=1, source_target_pairs={{0,4},{4,0},{8,12},{12,8},{1,5},{5,1},{9,13},{13,9},{2,6},{6,2},{1... | collective-permute-start | bytes 3293192 | tf_op jit(solution)/shard_map/ppermute | solution.py:38
  26.0 1.5 fusion.76
  27.6 2.2 %fusion.45 = (f32[128,1072]{0,1:T(8,128)S(1)}, f32[128,1072]{0,1:T(8,128)S(1)}) fusion(s32[128]{0:T(128)S(1)} %add_add_fusion.1, s32[1072]{0:T(1024)S(1)} %copy-done.30), kind=kLoop, calls=%fused_computation.83 | loop fusion | flops 2058240 | bytes 1102528 | tf_op jit(solution)/shard_map/cos | solution.py:46
  29.8 20.5 %collective-permute-done.2 = bf16[2,2,128,1072]{2,3,1,0:T(8,128)(2,1)S(1)} collective-permute-done((bf16[2,2,128,1072]{2,3,1,0:T(8,128)(2,1)S(1)}, bf16[2,2,128,1072]{2,3,1,0:T(8,128)(2,1)S(1)}, u32[]{:S(2)}, u32[]{:S(2)}) %collective-permute-start.2) | collective-permute-done | bytes 1097760 | tf_op jit(solution)/shard_map/ppermute | solution.py:38
  50.4 5.8 %select_bitcast_fusion.1 = (bf16[2,2,128,1072,1]{2,3,1,0,4:T(8,128)(2,1)S(1)}, bf16[2,2,128,1072,1]{2,3,1,0,4:T(8,128)(2,1)S(1)}) fusion(bf16[2,2,128,1072]{2,3,1,0:T(8,128)(2,1)S(1)} %collective-permute-done.2, pred[]{:T(512)S(6)} %eq.70, bf16[2,2,128,1088]{2,3,1,0:T(8,128)(2,1)S(1)} %pad_maximum_fusion, f32[128]{0:T(128)} %copy-done.35, f32[128]{0:T(128)} %copy-done.36, ...), kind=kLoop, calls=%fused_computation.32 | loop fusion | flops 29089792 | bytes 21963264 | tf_op jit(solution)/shard_map/jit(_where)/select_n | solution.py:122
  58.7 4.8 %add_convert_fusion.1 = bf16[2,2,128,1056]{2,3,0,1:T(8,128)(2,1)S(1)} fusion(bf16[2,2,128,1072]{2,3,0,1:T(8,128)(2,1)S(1)} %fusion.6, f32[128]{0:T(128)S(1)} %get-tuple-element.118, f32[128]{0:T(128)S(1)} %get-tuple-element.119, f32[128]{0:T(128)S(1)} %get-tuple-element.120, f32[128]{0:T(128)S(1)} %get-tuple-element.121, f32[128]{0:T(128)S(1)} %get-tuple-element.122, ...), kind=kLoop, calls=%fused_computation.17 | loop fusion | flops 27574272 | bytes 19472896 | tf_op jit(solution)/shard_map/convert_element_type | solution.py:78
  63.5 3.5 %collective-permute-start.3 = (bf16[2,2,128,1056]{2,3,0,1:T(8,128)(2,1)S(1)}, bf16[2,2,128,1056]{2,3,0,1:T(8,128)(2,1)S(1)}, u32[]{:S(2)}, u32[]{:S(2)}) collective-permute-start(bf16[2,2,128,1056]{2,3,0,1:T(8,128)(2,1)S(1)} %add_convert_fusion.1), channel_id=1, source_target_pairs={{0,8},{4,12},{8,0},{12,4},{1,9},{5,13},{9,1},{13,5},{2,10},{6,14},... | collective-permute-start | bytes 3244040 | tf_op jit(solution)/shard_map/ppermute | solution.py:38
  67.5 2.2 %fusion.47 = (f32[128,1056]{0,1:T(8,128)S(1)}, f32[128,1056]{0,1:T(8,128)S(1)}) fusion(s32[128]{0:T(128)S(1)} %add_add_fusion, s32[1056]{0:T(1024)S(1)} %copy-done.28), kind=kLoop, calls=%fused_computation.85 | loop fusion | flops 2027520 | bytes 1086080 | tf_op jit(solution)/shard_map/cos | solution.py:46
  69.7 44.7 %collective-permute-done.3 = bf16[2,2,128,1056]{2,3,0,1:T(8,128)(2,1)S(1)} collective-permute-done((bf16[2,2,128,1056]{2,3,0,1:T(8,128)(2,1)S(1)}, bf16[2,2,128,1056]{2,3,0,1:T(8,128)(2,1)S(1)}, u32[]{:S(2)}, u32[]{:S(2)}) %collective-permute-start.3) | collective-permute-done | bytes 1081376 | tf_op jit(solution)/shard_map/ppermute | solution.py:38
  116.9 4.6 %add_convert_fusion.2 = bf16[2,2,128,1040]{2,3,0,1:T(8,128)(2,1)S(1)} fusion(bf16[2,2,128,1056]{2,3,0,1:T(8,128)(2,1)S(1)} %fusion.7, f32[128]{0:T(128)S(1)} %get-tuple-element.101, f32[128]{0:T(128)S(1)} %get-tuple-element.102, f32[128]{0:T(128)S(1)} %get-tuple-element.103, f32[128]{0:T(128)S(1)} %get-tuple-element.104, f32[128]{0:T(128)S(1)} %get-tuple-element.105, ...), kind=kLoop, calls=%fused_computation.20 | loop fusion | flops 27156480 | bytes 19177984 | tf_op jit(solution)/shard_map/convert_element_type | solution.py:78
  121.4 0.8 collective-permute-start.4
  122.3 2.2 %fusion.49 = (f32[128,1040]{0,1:T(8,128)S(1)}, f32[128,1040]{0,1:T(8,128)S(1)}) fusion(s32[128]{0:T(128)S(1)} %copy-done.62, s32[1040]{0:T(1024)S(1)} %copy-done.29), kind=kLoop, calls=%fused_computation.87 | loop fusion | flops 1996800 | bytes 1069632 | tf_op jit(solution)/shard_map/cos | solution.py:46
  124.5 22.0 %collective-permute-done.4 = bf16[2,2,128,1040]{2,3,0,1:T(8,128)(2,1)S(1)} collective-permute-done((bf16[2,2,128,1040]{2,3,0,1:T(8,128)(2,1)S(1)}, bf16[2,2,128,1040]{2,3,0,1:T(8,128)(2,1)S(1)}, u32[]{:S(2)}, u32[]{:S(2)}) %collective-permute-start.4) | collective-permute-done | bytes 1064992 | tf_op jit(solution)/shard_map/ppermute | solution.py:38
  148.5 4.7 %add_convert_fusion.3 = bf16[2,2,128,1024]{2,3,0,1:T(8,128)(2,1)S(1)} fusion(bf16[2,2,128,1040]{2,3,0,1:T(8,128)(2,1)S(1)} %fusion.8, f32[128]{0:T(128)S(1)} %get-tuple-element.84, f32[128]{0:T(128)S(1)} %get-tuple-element.85, f32[128]{0:T(128)S(1)} %get-tuple-element.86, f32[128]{0:T(128)S(1)} %get-tuple-element.87, f32[128]{0:T(128)S(1)} %get-tuple-element.88, ...), kind=kLoop, calls=%fused_computation.25 | loop fusion | flops 26738688 | bytes 18883072 | tf_op jit(solution)/shard_map/convert_element_type | solution.py:78
  153.3 2.9 %collective-permute-start.5 = (bf16[2,2,128,1024]{2,3,0,1:T(8,128)(2,1)S(1)}, bf16[2,2,128,1024]{2,3,0,1:T(8,128)(2,1)S(1)}, u32[]{:S(2)}, u32[]{:S(2)}) collective-permute-start(bf16[2,2,128,1024]{2,3,0,1:T(8,128)(2,1)S(1)} %add_convert_fusion.3), channel_id=1, source_target_pairs={{0,8},{4,12},{8,0},{12,4},{1,9},{5,13},{9,1},{13,5},{2,10},{6,14},... | collective-permute-start | bytes 3145736 | tf_op jit(solution)/shard_map/ppermute | solution.py:38
  156.3 2.1 %fusion.51 = (f32[128,1024]{0,1:T(8,128)S(1)}, f32[128,1024]{0,1:T(8,128)S(1)}) fusion(s32[128]{0:T(128)S(1)} %add_add_fusion, s32[1024]{0:T(1024)S(1)} %iota_add_fusion.11), kind=kLoop, calls=%fused_computation.89 | loop fusion | flops 1966080 | bytes 1053184 | tf_op jit(solution)/shard_map/cos | solution.py:46
  158.4 43.0 %collective-permute-done.5 = bf16[2,2,128,1024]{2,3,0,1:T(8,128)(2,1)S(1)} collective-permute-done((bf16[2,2,128,1024]{2,3,0,1:T(8,128)(2,1)S(1)}, bf16[2,2,128,1024]{2,3,0,1:T(8,128)(2,1)S(1)}, u32[]{:S(2)}, u32[]{:S(2)}) %collective-permute-start.5) | collective-permute-done | bytes 1048608 | tf_op jit(solution)/shard_map/ppermute | solution.py:38
  203.1 1.3 copy.13
  (192 shorter events, 17.3 us)
Async XLA Ops:
  1.7 15.4 %collective-permute-start.1 = (bf16[2,2,128,32]{2,3,1,0:T(8,128)(2,1)S(1)}, bf16[2,2,128,32]{2,3,1,0:T(8,128)(2,1)S(1)}, u32[]{:S(2)}, u32[]{:S(2)}) collective-permute-start(bf16[2,2,128,32]{2,3,1,0:T(8,128)(2,1)S(1)} %get-tuple-element.50), channel_id=1, source_target_pairs={{1,0},{2,1},{3,2},{5,4},{6,5},{7,6},{9,8},{10,9},{11,10},{13,12},{... | collective-permute-start | bytes 98312 | tf_op jit(solution)/shard_map/ppermute | solution.py:28
  3.0 14.2 %collective-permute-start = (bf16[2,2,128,32]{2,3,1,0:T(8,128)(2,1)S(1)}, bf16[2,2,128,32]{2,3,1,0:T(8,128)(2,1)S(1)}, u32[]{:S(2)}, u32[]{:S(2)}) collective-permute-start(bf16[2,2,128,32]{2,3,1,0:T(8,128)(2,1)S(1)} %get-tuple-element.49), channel_id=1, source_target_pairs={{0,1},{1,2},{2,3},{4,5},{5,6},{6,7},{8,9},{9,10},{10,11},{12,13},{... | collective-permute-start | bytes 98312 | tf_op jit(solution)/shard_map/ppermute | solution.py:26
  6.2 10.9 %copy-start.2 = (bf16[1,2,2,2,128,128]{5,4,3,2,1,0:T(8,128)(2,1)}, bf16[1,2,2,2,128,128]{5,4,3,2,1,0:T(8,128)(2,1)S(1)}, u32[]{:S(2)}) copy-start(bf16[1,2,2,2,128,128]{5,4,3,2,1,0:T(8,128)(2,1)S(1)} %get-tuple-element.48) | copy-start | bytes 786436
  6.3 11.0 %copy-start.1 = (bf16[1,2,2,2,128,128]{5,4,3,2,1,0:T(8,128)(2,1)}, bf16[1,2,2,2,128,128]{5,4,3,2,1,0:T(8,128)(2,1)S(1)}, u32[]{:S(2)}) copy-start(bf16[1,2,2,2,128,128]{5,4,3,2,1,0:T(8,128)(2,1)S(1)} %get-tuple-element.45) | copy-start | bytes 786436
  12.5 10.1 %copy-start.36 = (f32[128]{0:T(128)}, f32[128]{0:T(128)S(1)}, u32[]{:S(2)}) copy-start(f32[128]{0:T(128)S(1)} %get-tuple-element.136) | copy-start | bytes 1540
  12.5 10.1 %copy-start.37 = (f32[128]{0:T(128)}, f32[128]{0:T(128)S(1)}, u32[]{:S(2)}) copy-start(f32[128]{0:T(128)S(1)} %get-tuple-element.137) | copy-start | bytes 1540
  17.8 32.5 %copy-start.43 = (f32[128]{0:T(128)S(1)}, f32[128]{0:T(128)}, u32[]{:S(2)}) copy-start(f32[128]{0:T(128)} %get-tuple-element.142) | copy-start | bytes 1540
  17.9 32.5 %copy-start.45 = (f32[128]{0:T(128)S(1)}, f32[128]{0:T(128)}, u32[]{:S(2)}) copy-start(f32[128]{0:T(128)} %get-tuple-element.143) | copy-start | bytes 1540
  17.9 32.5 %copy-start.47 = (f32[128]{0:T(128)S(1)}, f32[128]{0:T(128)}, u32[]{:S(2)}) copy-start(f32[128]{0:T(128)} %get-tuple-element.144) | copy-start | bytes 1540
  17.9 32.5 %copy-start.49 = (f32[128]{0:T(128)S(1)}, f32[128]{0:T(128)}, u32[]{:S(2)}) copy-start(f32[128]{0:T(128)} %get-tuple-element.145) | copy-start | bytes 1540
  17.9 32.5 %copy-start.51 = (f32[128]{0:T(128)S(1)}, f32[128]{0:T(128)}, u32[]{:S(2)}) copy-start(f32[128]{0:T(128)} %get-tuple-element.146) | copy-start | bytes 1540
  17.9 32.5 %copy-start.53 = (f32[128]{0:T(128)S(1)}, f32[128]{0:T(128)}, u32[]{:S(2)}) copy-start(f32[128]{0:T(128)} %get-tuple-element.147) | copy-start | bytes 1540
  17.9 32.5 %copy-start.55 = (f32[128]{0:T(128)S(1)}, f32[128]{0:T(128)}, u32[]{:S(2)}) copy-start(f32[128]{0:T(128)} %get-tuple-element.148) | copy-start | bytes 1540
  17.9 32.5 %copy-start.57 = (f32[128]{0:T(128)S(1)}, f32[128]{0:T(128)}, u32[]{:S(2)}) copy-start(f32[128]{0:T(128)} %get-tuple-element.149) | copy-start | bytes 1540
  17.9 32.5 %copy-start.59 = (f32[128]{0:T(128)S(1)}, f32[128]{0:T(128)}, u32[]{:S(2)}) copy-start(f32[128]{0:T(128)} %get-tuple-element.150) | copy-start | bytes 1540
  22.7 27.6 %collective-permute-start.2 = (bf16[2,2,128,1072]{2,3,1,0:T(8,128)(2,1)S(1)}, bf16[2,2,128,1072]{2,3,1,0:T(8,128)(2,1)S(1)}, u32[]{:S(2)}, u32[]{:S(2)}) collective-permute-start(bf16[2,2,128,1072]{2,3,1,0:T(8,128)(2,1)S(1)} %add_convert_fusion), channel_id=1, source_target_pairs={{0,4},{4,0},{8,12},{12,8},{1,5},{5,1},{9,13},{13,9},{2,6},{6,2},{1... | collective-permute-start | bytes 3293192 | tf_op jit(solution)/shard_map/ppermute | solution.py:38
  25.9 30.4 %copy-start.61 = (s32[128]{0:T(128)}, s32[128]{0:T(128)S(1)}, u32[]{:S(2)}) copy-start(s32[128]{0:T(128)S(1)} %add_add_fusion.1) | copy-start | bytes 1540
  29.8 26.5 %copy-start.15 = (bf16[1,2,128,128]{3,2,1,0:T(8,128)(2,1)S(1)}, bf16[1,2,128,128]{3,2,1,0:T(8,128)(2,1)}, u32[]{:S(2)}) copy-start(bf16[1,2,128,128]{3,2,1,0:T(8,128)(2,1)} %get-tuple-element.81) | copy-start | bytes 196612
  29.8 26.5 %copy-start.16 = (bf16[1,2,128,128]{3,2,1,0:T(8,128)(2,1)S(1)}, bf16[1,2,128,128]{3,2,1,0:T(8,128)(2,1)}, u32[]{:S(2)}) copy-start(bf16[1,2,128,128]{3,2,1,0:T(8,128)(2,1)} %get-tuple-element.82) | copy-start | bytes 196612
  58.7 55.7 %copy-start.3 = (bf16[1,2,128,128]{3,2,1,0:T(8,128)(2,1)S(1)}, bf16[1,2,128,128]{3,2,1,0:T(8,128)(2,1)}, u32[]{:S(2)}) copy-start(bf16[1,2,128,128]{3,2,1,0:T(8,128)(2,1)} %get-tuple-element.77) | copy-start | bytes 196612
  58.7 55.7 %copy-start.4 = (bf16[1,2,128,128]{3,2,1,0:T(8,128)(2,1)S(1)}, bf16[1,2,128,128]{3,2,1,0:T(8,128)(2,1)}, u32[]{:S(2)}) copy-start(bf16[1,2,128,128]{3,2,1,0:T(8,128)(2,1)} %get-tuple-element.78) | copy-start | bytes 196612
  63.5 50.9 %collective-permute-start.3 = (bf16[2,2,128,1056]{2,3,0,1:T(8,128)(2,1)S(1)}, bf16[2,2,128,1056]{2,3,0,1:T(8,128)(2,1)S(1)}, u32[]{:S(2)}, u32[]{:S(2)}) collective-permute-start(bf16[2,2,128,1056]{2,3,0,1:T(8,128)(2,1)S(1)} %add_convert_fusion.1), channel_id=1, source_target_pairs={{0,8},{4,12},{8,0},{12,4},{1,9},{5,13},{9,1},{13,5},{2,10},{6,14},... | collective-permute-start | bytes 3244040 | tf_op jit(solution)/shard_map/ppermute | solution.py:38
  121.4 25.0 %collective-permute-start.4 = (bf16[2,2,128,1040]{2,3,0,1:T(8,128)(2,1)S(1)}, bf16[2,2,128,1040]{2,3,0,1:T(8,128)(2,1)S(1)}, u32[]{:S(2)}, u32[]{:S(2)}) collective-permute-start(bf16[2,2,128,1040]{2,3,0,1:T(8,128)(2,1)S(1)} %add_convert_fusion.2), channel_id=1, source_target_pairs={{0,4},{4,0},{8,12},{12,8},{1,5},{5,1},{9,13},{13,9},{2,6},{6,2},{1... | collective-permute-start | bytes 3194888 | tf_op jit(solution)/shard_map/ppermute | solution.py:38
  153.3 48.2 %collective-permute-start.5 = (bf16[2,2,128,1024]{2,3,0,1:T(8,128)(2,1)S(1)}, bf16[2,2,128,1024]{2,3,0,1:T(8,128)(2,1)S(1)}, u32[]{:S(2)}, u32[]{:S(2)}) collective-permute-start(bf16[2,2,128,1024]{2,3,0,1:T(8,128)(2,1)S(1)} %add_convert_fusion.3), channel_id=1, source_target_pairs={{0,8},{4,12},{8,0},{12,4},{1,9},{5,13},{9,1},{13,5},{2,10},{6,14},... | collective-permute-start | bytes 3145736 | tf_op jit(solution)/shard_map/ppermute | solution.py:38
  (46 other events, 257.1 us)
where the time goes:
time: 205 us; the launch traced here: 204 us
  waiting for transfers between devices  130 us (63%)
  other arithmetic  46.6 us (23%)
  starting transfers between devices  14.7 us (7%)
  local copies, waits for them, and re-layouts  7.68 us (4%)
  matrix products  4.05 us (2%)
    ppermute x4, waiting for transfers between devices, from_partner(): return lax.ppermute(value, axis, pairs)  130 us
    convert_element_type x4, other arithmetic, interpolate(): return total.astype(jnp.bfloat16)  18.8 us
    ppermute x4, starting transfers between devices, from_partner(): return lax.ppermute(value, axis, pairs)  10.4 us
    cos x4, other arithmetic, rotate(): cosine = jnp.cos(phase)  8.68 us
    select_n x1, other arithmetic, on_device(): lower_rows = jnp.where(own_half == 0, own_rows, partner)  5.82 us
    unnamed x129, local copies, waits for them, and re-layouts  4.3 us
  transfers between devices with their start and end apart: 6, of which 4 were waited for; matrix products, arithmetic and copies ran while one was open for 11% of the time, Pallas kernels for 0%

commit v1 on v0

--- a/solution.py
+++ b/solution.py
@@ -1,8 +1,13 @@
 import math
+
+import functools
 
 import jax
 import jax.numpy as jnp
+import numpy as np
 from jax import lax
+from jax.experimental import pallas as pl
+from jax.experimental.pallas import tpu as pltpu
 from jax.sharding import PartitionSpec as P
 
 ANGLES = 128
@@ -130,9 +135,321 @@
     return current
 
 
+PERIOD = 64
+LANES = 128
+HALO = LEVELS * RIM
+MESH = pl.DeviceIdType.MESH
+NT = (((1,), (1,)), ((), ()))
+
+
+def phase_tables():
+    a = np.arange(ANGLES)
+    tables = np.zeros((LEVELS, 2, 2, PERIOD, ANGLES), np.float32)
+    for level in range(LEVELS):
+        for half in range(2):
+            start = -HALO if level < LEVELS - 1 else 0
+            r = (start + np.arange(PERIOD))[:, None]
+            wrapped = (r * (half * ANGLES + a + 1)[None, :] * (7 + level)) % PERIOD
+            phase = wrapped * phase_step
+            tables[level, half, 0] = np.cos(phase)
+            tables[level, half, 1] = np.sin(phase)
+    last = np.swapaxes(tables[LEVELS - 1], -1, -2)
+    last = np.concatenate([last] * (LANES // PERIOD), -1)
+    return tables[: LEVELS - 1], last
+
+
+def merge_kernel(
+    n, rngs, image, weights, taps, shifts, rows_table, cols_table, out,
+    xt, xin, big, table, xf, sh0, sh1, sh2, ybuf, stage,
+    in_send, in_recv, left_send, left_recv, right_send, right_recv, out_send, out_recv,
+):
+    me = lax.axis_index("sub")
+    place = lax.axis_index("rng")
+    groups, width = image.shape[1], image.shape[3]
+    block = width // n
+    rows = block + 2 * HALO
+    bits = n.bit_length() - 1
+
+    def span(z):
+        lo, hi = max(z * block - HALO, 0), min((z + 1) * block + HALO, width)
+        return lo, lo - (z * block - HALO), hi - lo
+
+    def in_copy(g, src, z):
+        lo, off, size = span(z)
+        return pltpu.make_async_remote_copy(
+            src_ref=xt.at[g, :, pl.ds(lo, size), :],
+            dst_ref=xin.at[g, src, :, pl.ds(off, size), :],
+            send_sem=in_send.at[g, z],
+            recv_sem=in_recv.at[g, src],
+            device_id={"sub": z},
+            device_id_type=MESH,
+        )
+
+    def left_copy(g, src):
+        return pltpu.make_async_remote_copy(
+            src_ref=xt.at[g, :, pl.ds(width - HALO, HALO), :],
+            dst_ref=xin.at[g, src, :, pl.ds(0, HALO), :],
+            send_sem=left_send.at[g],
+            recv_sem=left_recv.at[g, src],
+            device_id={"sub": 0, "rng": place + 1},
+            device_id_type=MESH,
+        )
+
+    def right_copy(g, src):
+        return pltpu.make_async_remote_copy(
+            src_ref=xt.at[g, :, pl.ds(0, HALO), :],
+            dst_ref=xin.at[g, src, :, pl.ds(rows - HALO, HALO), :],
+            send_sem=right_send.at[g],
+            recv_sem=right_recv.at[g, src],
+            device_id={"sub": n - 1, "rng": place - 1},
+            device_id_type=MESH,
+        )
+
+    def out_copy(g, z, owner):
+        return pltpu.make_async_remote_copy(
+            src_ref=stage.at[g, z],
+            dst_ref=out.at[:, g, :, pl.ds(pl.multiple_of(owner * block, LANES), block)],
+            send_sem=out_send.at[g, z],
+            recv_sem=out_recv.at[g, owner],
+            device_id={"sub": z},
+            device_id_type=MESH,
+        )
+
+    eye = (
+        lax.broadcasted_iota(jnp.int32, (LANES, LANES), 0)
+        == lax.broadcasted_iota(jnp.int32, (LANES, LANES), 1)
+    ).astype(jnp.bfloat16)
+
+    for g in range(groups):
+        for c in range(2):
+            for k in range(width // LANES):
+                cols = pl.ds(k * LANES, LANES)
+                xt[g, c, cols, :] = lax.dot_general(
+                    eye, image[c, g, :, cols], NT, preferred_element_type=jnp.float32
+                ).astype(jnp.bfloat16)
+        for z in range(n):
+
+            @pl.when(me != z)
+            def _():
+                in_copy(g, me, z).start()
+
+        @pl.when(place < rngs - 1)
+        def _():
+            left_copy(g, me).start()
+
+        @pl.when(place > 0)
+        def _():
+            right_copy(g, me).start()
+
+    at_left = jnp.logical_and(place == 0, me == 0)
+    at_right = jnp.logical_and(place == rngs - 1, me == n - 1)
+
+    for z in range(n):
+
+        @pl.when(me == z)
+        def _():
+            lo, off, size = span(z)
+            for g in range(groups):
+                xin[g, z, :, off : off + size, :] = xt[g, :, lo : lo + size, :]
+
+    @pl.when(at_left)
+    def _():
+        xin[:, :, :, :HALO, :] = jnp.zeros((groups, n, 2, HALO, ANGLES), jnp.bfloat16)
+
+    @pl.when(at_right)
+    def _():
+        xin[:, :, :, rows - HALO :, :] = jnp.zeros((groups, n, 2, HALO, ANGLES), jnp.bfloat16)
+
+    for level in range(LEVELS):
+        for half in range(2):
+            for side in range(2):
+                real = weights[level, side, half, 0]
+                imag = weights[level, side, half, 1]
+                i = half * 2 * ANGLES
+                j = side * 2 * ANGLES
+                big[level, i : i + ANGLES, j : j + ANGLES] = real
+                big[level, i : i + ANGLES, j + ANGLES : j + 2 * ANGLES] = -imag
+                big[level, i + ANGLES : i + 2 * ANGLES, j : j + ANGLES] = imag
+                big[level, i + ANGLES : i + 2 * ANGLES, j + ANGLES : j + 2 * ANGLES] = real
+            if level < LEVELS - 1:
+                for part in range(2):
+                    for start in range(0, rows, PERIOD):
+                        size = min(PERIOD, rows - start)
+                        table[level, half, part, start : start + size, :] = rows_table[
+                            level, half, part, :size, :
+                        ]
+
+    def per_group(g, carry):
+        for z in range(n):
+
+            @pl.when(me == z)
+            def _():
+                for src in range(n):
+                    if src != z:
+                        in_copy(g, src, z).wait_recv()
+
+        @pl.when(jnp.logical_and(me == 0, place > 0))
+        def _():
+            for src in range(n):
+                left_copy(g, src).wait_recv()
+
+        @pl.when(jnp.logical_and(me == n - 1, place < rngs - 1))
+        def _():
+            for src in range(n):
+                right_copy(g, src).wait_recv()
+
+        for s in range(n):
+            for c in range(2):
+                xf[s, c, :rows, :] = xin[g, s, c].astype(jnp.float32)
+
+        for level in range(LEVELS):
+            mask = 2 ** (level % bits)
+            base = RIM * level
+            count = rows - 2 * base
+            kept = count - 2 * RIM
+            wide = kept + RIM
+
+            def per_pair(pair, inner, level=level, mask=mask, base=base, count=count, kept=kept, wide=wide):
+                low = pair // mask * (2 * mask) + pair % mask
+                members = (low, low + mask)
+                for side in range(2):
+                    k = shifts[level, side][None, :] + RIM
+                    on8, on4, on2, on1 = [(k // p) % 2 == 1 for p in (8, 4, 2, 1)]
+                    for c in range(2):
+                        s = members[side]
+                        u = None
+                        for t in range(TAPS):
+                            term = taps[level, t] * xf[s, c, pl.ds(base + t, count), :]
+                            u = term if u is None else u + term
+                        v = jnp.where(on8, u[RIM:], u[:wide])
+                        sh0[:wide] = v
+                        v = jnp.where(on4, sh0[pl.ds(4, wide), :], v)
+                        sh1[:wide] = v
+                        v = jnp.where(on2, sh1[pl.ds(2, wide), :], v)
+                        sh2[:wide] = v
+                        v = jnp.where(on1, sh2[pl.ds(1, kept), :], v[:kept])
+                        j = (side * 2 + c) * ANGLES
+                        ybuf[:kept, j : j + ANGLES] = v.astype(jnp.bfloat16)
+                y = ybuf[:kept, :]
+                if level < LEVELS - 1:
+                    z = lax.dot_general(y, big[level], NT, preferred_element_type=jnp.float32)
+                    for half in range(2):
+                        s = members[half]
+                        j = half * 2 * ANGLES
+                        re, im = z[:, j : j + ANGLES], z[:, j + ANGLES : j + 2 * ANGLES]
+                        span_rows = pl.ds(base + RIM, kept)
+                        cosine = table[level, half, 0, span_rows, :]
+                        sinus = table[level, half, 1, span_rows, :]
+                        xf[s, 0, span_rows, :] = re * cosine - im * sinus
+                        xf[s, 1, span_rows, :] = re * sinus + im * cosine
+                else:
+                    z = lax.dot_general(big[level], y, NT, preferred_element_type=jnp.float32)
+                    for half in range(2):
+                        s = members[half]
+                        i = half * 2 * ANGLES
+                        cosine, sinus = cols_table[half, 0], cols_table[half, 1]
+                        for start in range(0, block, LANES):
+                            cols = slice(start, start + LANES)
+                            re, im = z[i : i + ANGLES, cols], z[i + ANGLES : i + 2 * ANGLES, cols]
+                            stage[g, s, 0, :, cols] = (re * cosine - im * sinus).astype(jnp.bfloat16)
+                            stage[g, s, 1, :, cols] = (re * sinus + im * cosine).astype(jnp.bfloat16)
+                return inner
+
+            lax.fori_loop(0, n // 2, per_pair, 0)
+            if level < LEVELS - 1:
+
+                @pl.when(at_left)
+                def _():
+                    xf[:, :, :HALO, :] = jnp.zeros((n, 2, HALO, ANGLES), jnp.float32)
+
+                @pl.when(at_right)
+                def _():
+                    xf[:, :, rows - HALO : rows, :] = jnp.zeros((n, 2, HALO, ANGLES), jnp.float32)
+
+        for z in range(n):
+
+            @pl.when(me != z)
+            def _():
+                out_copy(g, z, me).start()
+
+            @pl.when(me == z)
+            def _():
+                out[:, g, :, z * block : (z + 1) * block] = stage[g, z]
+
+        return carry
+
+    lax.fori_loop(0, groups, per_group, 0)
+
+    for g in range(groups):
+        for z in range(n):
+
+            @pl.when(me != z)
+            def _():
+                in_copy(g, me, z).wait_send()
+                out_copy(g, z, me).wait_send()
+                out_copy(g, z, z).wait_recv()
+
+        @pl.when(place < rngs - 1)
+        def _():
+            left_copy(g, me).wait_send()
+
+        @pl.when(place > 0)
+        def _():
+            right_copy(g, me).wait_send()
+
+
+def in_one_kernel(n, rngs, image, interp_weights, range_taps, range_shifts):
+    groups, width = image.shape[1], image.shape[3]
+    block = width // n
+    rows = block + 2 * HALO
+    rows_table, cols_table = phase_tables()
+    vmem = pl.BlockSpec(memory_space=pltpu.VMEM)
+    dma = pltpu.SemaphoreType.DMA
+    f32, bf16 = jnp.float32, jnp.bfloat16
+    return pl.pallas_call(
+        functools.partial(merge_kernel, n, rngs),
+        out_shape=jax.ShapeDtypeStruct(image.shape, bf16),
+        in_specs=[vmem, vmem, pl.BlockSpec(memory_space=pltpu.SMEM), vmem, vmem, vmem],
+        out_specs=vmem,
+        scratch_shapes=[
+            pltpu.VMEM((groups, 2, width, ANGLES), bf16),
+            pltpu.VMEM((groups, n, 2, rows, ANGLES), bf16),
+            pltpu.VMEM((LEVELS, 4 * ANGLES, 4 * ANGLES), bf16),
+            pltpu.VMEM((LEVELS - 1, 2, 2, rows, ANGLES), f32),
+            pltpu.VMEM((n, 2, rows + 8, ANGLES), f32),
+            pltpu.VMEM((rows + 8, ANGLES), f32),
+            pltpu.VMEM((rows + 8, ANGLES), f32),
+            pltpu.VMEM((rows + 8, ANGLES), f32),
+            pltpu.VMEM((rows, 4 * ANGLES), bf16),
+            pltpu.VMEM((groups, n, 2, ANGLES, block), bf16),
+            dma((groups, n)),
+            dma((groups, n)),
+            dma((groups,)),
+            dma((groups, n)),
+            dma((groups,)),
+            dma((groups, n)),
+            dma((groups, n)),
+            dma((groups, n)),
+        ],
+        compiler_params=pltpu.CompilerParams(has_side_effects=True),
+    )(image, interp_weights, range_taps, range_shifts, rows_table, cols_table)
+
+
+def fits_kernel(mesh, width):
+    n = mesh.shape["sub"]
+    block = width // n
+    return n > 1 and n & (n - 1) == 0 and block % LANES == 0 and block >= HALO and ANGLES == LANES
+
+
+def per_device(mesh, image, *rest):
+    if fits_kernel(mesh, image.shape[3]):
+        return in_one_kernel(mesh.shape["sub"], mesh.shape["rng"], image, *rest)
+    return on_device(image, *rest)
+
+
 def solution(mesh):
     return jax.shard_map(
-        on_device,
+        functools.partial(per_device, mesh),
         mesh=mesh,
         in_specs=(P(None, ("img", "sub"), None, "rng"), P(), P(), P()),
         out_specs=P(None, ("img", "sub"), None, "rng"),

time: 205 us -> 65.4 us (0.32)
  waiting for transfers between devices: 130 us -> 0 us
  Pallas kernels: 0 us -> 63 us
  other arithmetic: 46.6 us -> 0 us
  starting transfers between devices: 14.7 us -> 0 us
  local copies, waits for them, and re-layouts: 7.68 us -> 2.26 us
  matrix products: 4.05 us -> 0 us
    ppermute x6 -> x0, waiting for transfers between devices: 130 us -> none  [the longest x4 130 us: from_partner(): return lax.ppermute(value, axis, pairs)]
    pallas_call x0 -> x1, Pallas kernels: none -> 63 us  [in_one_kernel(): pl.pallas_call(functools.partial(merge_kernel, n, rngs), out_shape=jax.Sh...]
    convert_element_type x8 -> x0, other arithmetic: 20 us -> none  [the longest x4 18.8 us: interpolate(): return total.astype(jnp.bfloat16)]
    ppermute x6 -> x0, starting transfers between devices: 14.7 us -> none  [the longest x4 10.4 us: from_partner(): return lax.ppermute(value, axis, pairs)]
    cos x4 -> x0, other arithmetic: 8.68 us -> none  [rotate(): cosine = jnp.cos(phase)]
    select_n x5 -> x0, other arithmetic: 5.84 us -> none  [the longest x1 5.82 us: on_device(): lower_rows = jnp.where(own_half == 0, own_rows, partner)]
    dot_general x8 -> x0, matrix products: 4.05 us -> none  [combine_sides(): jnp.einsum('xcij,cgjr->xgir', block_of(chosen[side_index]), source, prefe...]
    another operation x8 -> x0, other arithmetic: 2.7 us -> none  [block_of(): jnp.stack([jnp.stack([weight_pair[0], -weight_pair[1]]), jnp.stack([weigh...]
  transfers between devices with their start and end apart: 6 -> 0, of which waited for: 4 -> 0; matrix products, arithmetic and copies ran while one was open for 11% -> 0% of each run, Pallas kernels for 0% -> 0%
where the time goes in v1:
time: 65.4 us; the launch traced here: 65.3 us
  Pallas kernels  63 us (96%)
  local copies, waits for them, and re-layouts  2.26 us (3%)
    pallas_call x1, Pallas kernels, in_one_kernel(): pl.pallas_call(functools.partial(merge_kernel, n, rngs), out_shape=jax.Sh...  63 us
    unnamed x1, local copies, waits for them, and re-layouts  2.26 us

profile of v1, /device:TPU:0, one launch (start us, length us, event | category | flops | bytes accessed | tf_op | source)
XLA Modules:
  0.0 65.3 jit_solution(2303463805689813378)
XLA Ops:
  0.0 63.0 %shard_map.64 = bf16[2,2,128,1024]{3,2,1,0:T(8,128)(2,1)} custom-call(bf16[2,2,128,1024]{3,2,1,0:T(8,128)(2,1)} %image.1, bf16[4,2,2,2,128,128]{5,4,3,2,1,0:T(8,128)(2,1)} %weights.1, f32[4,4]{1,0:T(4,128)} %taps.1, s32[4,2,128]{2,1,0:T(2,128)} %shifts.1, f32[3,2,2,64,128]{4,3,2,1,0:T(8,128)} %constant.4.clone.rows_table, ...), custom_call_target="tpu_custom_call" | custom-call | tf_op jit(solution)/shard_map/pallas_call | solution.py:409
  63.0 2.3 %copy.8 = bf16[2,2,128,1024]{3,2,1,0:T(8,128)(2,1)} copy(bf16[2,2,128,1024]{3,2,1,0:T(8,128)(2,1)} %shard_map.64) | data formatting | bytes 2097152

commit v2 on v1

--- a/solution.py
+++ b/solution.py
@@ -159,29 +159,47 @@
 
 
 def merge_kernel(
-    n, rngs, image, weights, taps, shifts, rows_table, cols_table, out,
+    n, rngs, image_hbm, weights_hbm, taps, shifts, rows_hbm, cols_hbm, out,
+    image, weights, rows_table, cols_table, load_sem,
     xt, xin, big, table, xf, sh0, sh1, sh2, ybuf, stage,
-    in_send, in_recv, left_send, left_recv, right_send, right_recv, out_send, out_recv,
+    in_send, in_recv, left_send, left_recv, right_send, right_recv, twin_send, twin_recv, out_send, out_recv,
 ):
     me = lax.axis_index("sub")
     place = lax.axis_index("rng")
-    groups, width = image.shape[1], image.shape[3]
+    groups, width = image_hbm.shape[1], image_hbm.shape[3]
     block = width // n
     rows = block + 2 * HALO
     bits = n.bit_length() - 1
 
-    def span(z):
-        lo, hi = max(z * block - HALO, 0), min((z + 1) * block + HALO, width)
-        return lo, lo - (z * block - HALO), hi - lo
-
-    def in_copy(g, src, z):
-        lo, off, size = span(z)
+    twin = place % 2
+    first = place - twin
+    mine = 2 * me + twin
+    near = (HALO, 0), (0, HALO)
+
+    def span(b):
+        start = b % n * block
+        lo = max(start - near[b % 2][0], 0)
+        hi = min(start + block + near[b % 2][1], width)
+        return lo, HALO + lo - start, hi - lo
+
+    def in_copy(g, src, b):
+        lo, off, size = span(b)
         return pltpu.make_async_remote_copy(
             src_ref=xt.at[g, :, pl.ds(lo, size), :],
             dst_ref=xin.at[g, src, :, pl.ds(off, size), :],
-            send_sem=in_send.at[g, z],
+            send_sem=in_send.at[g, b],
             recv_sem=in_recv.at[g, src],
-            device_id={"sub": z},
+            device_id={"sub": b // 2, "rng": first + b % 2},
+            device_id_type=MESH,
+        )
+
+    def twin_copy(g, size_from, size_to):
+        return pltpu.make_async_remote_copy(
+            src_ref=xin.at[g, :, :, pl.ds(size_from, HALO), :],
+            dst_ref=xin.at[g, :, :, pl.ds(size_to, HALO), :],
+            send_sem=twin_send.at[g],
+            recv_sem=twin_recv.at[g],
+            device_id={"rng": place + 1 - 2 * twin},
             device_id_type=MESH,
         )
 
@@ -191,7 +209,7 @@
             dst_ref=xin.at[g, src, :, pl.ds(0, HALO), :],
             send_sem=left_send.at[g],
             recv_sem=left_recv.at[g, src],
-            device_id={"sub": 0, "rng": place + 1},
+            device_id={"sub": (1 - twin) * (n // 2), "rng": first + 2 * twin},
             device_id_type=MESH,
         )
 
@@ -201,19 +219,54 @@
             dst_ref=xin.at[g, src, :, pl.ds(rows - HALO, HALO), :],
             send_sem=right_send.at[g],
             recv_sem=right_recv.at[g, src],
-            device_id={"sub": n - 1, "rng": place - 1},
+            device_id={"sub": twin * (n // 2) + (1 - twin) * n - 1, "rng": first - 1 + 2 * twin},
             device_id_type=MESH,
         )
 
     def out_copy(g, z, owner):
         return pltpu.make_async_remote_copy(
             src_ref=stage.at[g, z],
-            dst_ref=out.at[:, g, :, pl.ds(pl.multiple_of(owner * block, LANES), block)],
+            dst_ref=out.at[:, g, :, pl.ds(pl.multiple_of(owner % n * block, LANES), block)],
             send_sem=out_send.at[g, z],
-            recv_sem=out_recv.at[g, owner],
-            device_id={"sub": z},
+            recv_sem=out_recv.at[g, owner % n],
+            device_id={"sub": z, "rng": first + owner // n},
             device_id_type=MESH,
         )
+
+    left_self = jnp.logical_and(twin == 0, me == n // 2)
+    left_out = jnp.logical_and(jnp.logical_not(left_self), place < rngs - 1)
+    right_self = jnp.logical_and(twin == 1, me == n // 2 - 1)
+    right_out = jnp.logical_and(jnp.logical_not(right_self), place > 0)
+
+    head_from_left = jnp.logical_and(mine == 0, place > 0)
+    tail_from_right = jnp.logical_and(mine == 2 * n - 1, place < rngs - 1)
+    barrier = pltpu.get_barrier_semaphore()
+
+    def ready(cond, z, r):
+        @pl.when(cond)
+        def _():
+            pl.semaphore_signal(
+                barrier, inc=1, device_id={"sub": z, "rng": r}, device_id_type=MESH
+            )
+
+    for z in range(n):
+        for c in range(2):
+            ready(mine != 2 * z + c, z, first + c)
+        ready(head_from_left, z, place - 1)
+        ready(tail_from_right, z, place + 1)
+
+    loads = [
+        pltpu.make_async_copy(image_hbm.at[:, g], image.at[:, g], load_sem.at[g])
+        for g in range(groups)
+    ]
+    others = [
+        pltpu.make_async_copy(src, dst, load_sem.at[groups + k])
+        for k, (src, dst) in enumerate(
+            ((weights_hbm, weights), (rows_hbm, rows_table), (cols_hbm, cols_table))
+        )
+    ]
+    for copy in loads + others:
+        copy.start()
 
     eye = (
         lax.broadcasted_iota(jnp.int32, (LANES, LANES), 0)
@@ -221,36 +274,53 @@
     ).astype(jnp.bfloat16)
 
     for g in range(groups):
+        loads[g].wait()
         for c in range(2):
             for k in range(width // LANES):
                 cols = pl.ds(k * LANES, LANES)
                 xt[g, c, cols, :] = lax.dot_general(
                     eye, image[c, g, :, cols], NT, preferred_element_type=jnp.float32
                 ).astype(jnp.bfloat16)
-        for z in range(n):
-
-            @pl.when(me != z)
+        if g == 0:
+            sends_edge = jnp.where(twin == 1, place < rngs - 1, place > 0)
+            pl.semaphore_wait(barrier, 2 * n - 1 + sends_edge.astype(jnp.int32))
+
+        @pl.when(left_out)
+        def _():
+            left_copy(g, me).start()
+
+        @pl.when(right_out)
+        def _():
+            right_copy(g, me).start()
+
+        for b in range(2 * n):
+
+            @pl.when(jnp.logical_and(twin == b // n, mine != b))
             def _():
-                in_copy(g, me, z).start()
-
-        @pl.when(place < rngs - 1)
-        def _():
-            left_copy(g, me).start()
-
-        @pl.when(place > 0)
-        def _():
-            right_copy(g, me).start()
+                in_copy(g, me, b).start()
 
     at_left = jnp.logical_and(place == 0, me == 0)
     at_right = jnp.logical_and(place == rngs - 1, me == n - 1)
 
-    for z in range(n):
-
-        @pl.when(me == z)
-        def _():
-            lo, off, size = span(z)
-            for g in range(groups):
-                xin[g, z, :, off : off + size, :] = xt[g, :, lo : lo + size, :]
+    for b in range(2 * n):
+        z = b // 2
+        if b % 2 == b // n:
+
+            @pl.when(mine == b)
+            def _():
+                lo, off, size = span(b)
+                for g in range(groups):
+                    xin[g, z, :, off : off + size, :] = xt[g, :, lo : lo + size, :]
+
+    @pl.when(left_self)
+    def _():
+        for g in range(groups):
+            xin[g, n // 2, :, :HALO, :] = xt[g, :, width - HALO :, :]
+
+    @pl.when(right_self)
+    def _():
+        for g in range(groups):
+            xin[g, n // 2 - 1, :, rows - HALO :, :] = xt[g, :, :HALO, :]
 
     @pl.when(at_left)
     def _():
@@ -259,6 +329,9 @@
     @pl.when(at_right)
     def _():
         xin[:, :, :, rows - HALO :, :] = jnp.zeros((groups, n, 2, HALO, ANGLES), jnp.bfloat16)
+
+    for copy in others:
+        copy.wait()
 
     for level in range(LEVELS):
         for half in range(2):
@@ -279,24 +352,47 @@
                             level, half, part, :size, :
                         ]
 
+    def send_back(g, s):
+        here = jnp.logical_and(s == me, twin == mine // n)
+
+        @pl.when(jnp.logical_not(here))
+        def _():
+            out_copy(g, s, mine).start()
+
+        @pl.when(here)
+        def _():
+            out[:, g, :, pl.ds(pl.multiple_of(mine % n * block, LANES), block)] = stage[g, s]
+
     def per_group(g, carry):
-        for z in range(n):
-
-            @pl.when(me == z)
+        for b in range(2 * n):
+
+            @pl.when(mine == b)
             def _():
                 for src in range(n):
-                    if src != z:
-                        in_copy(g, src, z).wait_recv()
-
-        @pl.when(jnp.logical_and(me == 0, place > 0))
+                    if b % 2 != b // n or src != b // 2:
+                        in_copy(g, src, b).wait_recv()
+                if b % 2 == 0:
+                    twin_copy(g, block, 0).start()
+                else:
+                    twin_copy(g, HALO, rows - HALO).start()
+
+        @pl.when(jnp.logical_or(mine == n, jnp.logical_and(mine == 0, place > 0)))
         def _():
             for src in range(n):
-                left_copy(g, src).wait_recv()
-
-        @pl.when(jnp.logical_and(me == n - 1, place < rngs - 1))
+
+                @pl.when(jnp.logical_or(mine == 0, src != n // 2))
+                def _():
+                    left_copy(g, src).wait_recv()
+
+        @pl.when(jnp.logical_or(mine == n - 1, jnp.logical_and(mine == 2 * n - 1, place < rngs - 1)))
         def _():
             for src in range(n):
-                right_copy(g, src).wait_recv()
+
+                @pl.when(jnp.logical_or(mine == 2 * n - 1, src != n // 2 - 1))
+                def _():
+                    right_copy(g, src).wait_recv()
+
+        twin_copy(g, 0, 0).wait()
 
         for s in range(n):
             for c in range(2):
@@ -353,6 +449,9 @@
                             re, im = z[i : i + ANGLES, cols], z[i + ANGLES : i + 2 * ANGLES, cols]
                             stage[g, s, 0, :, cols] = (re * cosine - im * sinus).astype(jnp.bfloat16)
                             stage[g, s, 1, :, cols] = (re * sinus + im * cosine).astype(jnp.bfloat16)
+                    for half in range(2):
+                        send_back(g, members[half])
+
                 return inner
 
             lax.fori_loop(0, n // 2, per_pair, 0)
@@ -366,34 +465,32 @@
                 def _():
                     xf[:, :, rows - HALO : rows, :] = jnp.zeros((n, 2, HALO, ANGLES), jnp.float32)
 
+        return carry
+
+    lax.fori_loop(0, groups, per_group, 0)
+
+    for g in range(groups):
+        for b in range(2 * n):
+
+            @pl.when(jnp.logical_and(twin == b // n, mine != b))
+            def _():
+                in_copy(g, me, b).wait_send()
+
         for z in range(n):
 
-            @pl.when(me != z)
+            @pl.when(jnp.logical_not(jnp.logical_and(me == z, twin == mine // n)))
             def _():
-                out_copy(g, z, me).start()
-
-            @pl.when(me == z)
+                out_copy(g, z, mine).wait_send()
+
+            @pl.when(mine != n * twin + z)
             def _():
-                out[:, g, :, z * block : (z + 1) * block] = stage[g, z]
-
-        return carry
-
-    lax.fori_loop(0, groups, per_group, 0)
-
-    for g in range(groups):
-        for z in range(n):
-
-            @pl.when(me != z)
-            def _():
-                in_copy(g, me, z).wait_send()
-                out_copy(g, z, me).wait_send()
-                out_copy(g, z, z).wait_recv()
-
-        @pl.when(place < rngs - 1)
+                out_copy(g, z, n * twin + z).wait_recv()
+
+        @pl.when(left_out)
         def _():
             left_copy(g, me).wait_send()
 
-        @pl.when(place > 0)
+        @pl.when(right_out)
         def _():
             right_copy(g, me).wait_send()
 
@@ -404,14 +501,20 @@
     rows = block + 2 * HALO
     rows_table, cols_table = phase_tables()
     vmem = pl.BlockSpec(memory_space=pltpu.VMEM)
+    hbm = pl.BlockSpec(memory_space=pl.ANY)
     dma = pltpu.SemaphoreType.DMA
     f32, bf16 = jnp.float32, jnp.bfloat16
     return pl.pallas_call(
         functools.partial(merge_kernel, n, rngs),
         out_shape=jax.ShapeDtypeStruct(image.shape, bf16),
-        in_specs=[vmem, vmem, pl.BlockSpec(memory_space=pltpu.SMEM), vmem, vmem, vmem],
+        in_specs=[hbm, hbm, pl.BlockSpec(memory_space=pltpu.SMEM), vmem, hbm, hbm],
         out_specs=vmem,
         scratch_shapes=[
+            pltpu.VMEM(image.shape, bf16),
+            pltpu.VMEM(interp_weights.shape, bf16),
+            pltpu.VMEM(rows_table.shape, f32),
+            pltpu.VMEM(cols_table.shape, f32),
+            dma((groups + 3,)),
             pltpu.VMEM((groups, 2, width, ANGLES), bf16),
             pltpu.VMEM((groups, n, 2, rows, ANGLES), bf16),
             pltpu.VMEM((LEVELS, 4 * ANGLES, 4 * ANGLES), bf16),
@@ -422,23 +525,26 @@
             pltpu.VMEM((rows + 8, ANGLES), f32),
             pltpu.VMEM((rows, 4 * ANGLES), bf16),
             pltpu.VMEM((groups, n, 2, ANGLES, block), bf16),
-            dma((groups, n)),
+            dma((groups, 2 * n)),
             dma((groups, n)),
             dma((groups,)),
             dma((groups, n)),
             dma((groups,)),
             dma((groups, n)),
+            dma((groups,)),
+            dma((groups,)),
             dma((groups, n)),
             dma((groups, n)),
         ],
-        compiler_params=pltpu.CompilerParams(has_side_effects=True),
+        compiler_params=pltpu.CompilerParams(has_side_effects=True, collective_id=0),
     )(image, interp_weights, range_taps, range_shifts, rows_table, cols_table)
 
 
 def fits_kernel(mesh, width):
     n = mesh.shape["sub"]
     block = width // n
-    return n > 1 and n & (n - 1) == 0 and block % LANES == 0 and block >= HALO and ANGLES == LANES
+    paired = mesh.shape["rng"] % 2 == 0
+    return paired and n > 1 and n & (n - 1) == 0 and block % LANES == 0 and block >= HALO and ANGLES == LANES
 
 
 def per_device(mesh, image, *rest):

time: 65.4 us -> 59.7 us (0.913)
  the two profiles are of different devices: /device:TPU:0 before, /device:TPU:15 now
where the time goes in v2:
time: 59.7 us; the launch traced here: 59.6 us
  Pallas kernels  57.3 us (96%)
  local copies, waits for them, and re-layouts  2.26 us (4%)
    pallas_call x1, Pallas kernels, in_one_kernel(): pl.pallas_call(functools.partial(merge_kernel, n, rngs), out_shape=jax.Sh...  57.3 us
    unnamed x1, local copies, waits for them, and re-layouts  2.26 us

profile of v2, /device:TPU:15, one launch (start us, length us, event | category | flops | bytes accessed | tf_op | source)
XLA Modules:
  0.0 59.6 jit_solution(11071727029183447400)
XLA Ops:
  0.0 57.3 %shard_map.64 = bf16[2,2,128,1024]{3,2,1,0:T(8,128)(2,1)} custom-call(bf16[2,2,128,1024]{3,2,1,0:T(8,128)(2,1)} %image_hbm.1, bf16[4,2,2,2,128,128]{5,4,3,2,1,0:T(8,128)(2,1)} %weights_hbm.1, f32[4,4]{1,0:T(4,128)} %taps.1, s32[4,2,128]{2,1,0:T(2,128)} %shifts.1, f32[3,2,2,64,128]{4,3,2,1,0:T(8,128)} %constant.4.clone.rows_hbm, ...), custom_call_target="tpu_custom_call" | custom-call | tf_op jit(solution)/shard_map/pallas_call | solution.py:507
  57.3 2.3 %copy.8 = bf16[2,2,128,1024]{3,2,1,0:T(8,128)(2,1)} copy(bf16[2,2,128,1024]{3,2,1,0:T(8,128)(2,1)} %shard_map.64) | data formatting | bytes 2097152
